TPU v7x, 512 devices: a whole 4x8x8 slice. The times are simulated.
512 devices in a mesh: ma: 64 (over z, x, core), ba: 8 (over y).
Axes of the slice: x: 4, y: 8, z: 8, core: 2. Of those that a mesh axis runs over, the one named last changes fastest.
Arguments:
- fields: bfloat16 [16, 256, 256, 192], P('ba', 'ma'), may hold values from -6 to 6
- weight_real: bfloat16 [112, 64, 192, 192], P('ba', 'ma'), may hold values from -0.4375 to 0.4375
- weight_imag: bfloat16 [112, 64, 192, 192], P('ba', 'ma'), may hold values from -0.4375 to 0.4375
- skip_weight: bfloat16 [192, 192], replicated, may hold values from -0.4375 to 0.4375
- out_bias: float32 [192], replicated, may hold values from -3 to 3
Outputs:
- layer_out: bfloat16 [16, 256, 256, 192], P('ba', 'ma')
All inputs are finite; a program needn't handle non-finite values.
Results may differ from a plain program's by a relative error of at most 0.0095.
Values may be sent and summed in bfloat16 or wider, within the bound.
A program may use at most 64 MiB of HBM per device.

v0:
```python
import functools
import math

import jax
import jax.numpy as jnp
import numpy as np
from jax import lax
from jax.experimental import pallas as pl
from jax.experimental.pallas import tpu as pltpu
from jax.sharding import PartitionSpec as P

MESH = pl.DeviceIdType.MESH
BF = jnp.bfloat16
F32 = jnp.float32
LANES = 128
VMEM_LIMIT = 67043328


def angles(left, right, extent):
    turn = 2.0 * np.pi / extent * ((left[:, None] * right[None, :]) % extent)
    return np.cos(turn), np.sin(turn)


def packed_tables(H, W, KX, KY, n, nb):
    rows, cols, modes = H // n, KY // n, KX // nb
    s = 1.0 / math.sqrt(H * W)
    ky = np.arange(KY)
    cos_w, sin_w = angles(ky, np.arange(W), W)
    first = np.stack([cos_w * s, -sin_w * s], 1)
    first = first.reshape(n, cols, 2, W).transpose(1, 0, 2, 3).reshape(2 * KY, W)
    g = np.where(ky == 0, 1.0, 2.0)[:, None] * s
    last = np.stack([cos_w * g, -sin_w * g], 1)
    last = last.reshape(n, cols, 2, W).transpose(1, 0, 2, 3).reshape(2 * KY, W)
    i = np.arange(KX)
    kx = np.where(i < KX // 2, i, i + H - KX)
    cos_h, sin_h = angles(kx, np.arange(H), H)
    down = np.stack([np.stack([cos_h, sin_h], 1), np.stack([-sin_h, cos_h], 1)], 0)
    down = down.reshape(2, nb, modes, 2, n, rows).transpose(1, 0, 2, 4, 3, 5)
    down = down.reshape(2 * KX, 2 * H)
    up = np.stack([np.stack([cos_h, -sin_h], 0), np.stack([sin_h, cos_h], 0)], 0)
    up = up.reshape(2, 2, nb, modes, n, rows).transpose(4, 0, 5, 2, 1, 3).reshape(2 * H, 2 * KX)
    return [jnp.asarray(a.astype(np.float32)).astype(BF) for a in (first, down, up, last)]


def dot(a, b, over=(1, 0)):
    return lax.dot_general(a, b, (((over[0],), (over[1],)), ((), ())), preferred_element_type=F32)


def spectral_kernel(
    n, nb, x_ref, wr_ref, wi_ref, first_ref, down_ref, up_ref, out_ref,
    colf, csend, crecv, ysend, yrecv, m1, m2, mo, zsend, zrecv, rsend, wbuf,
    csem_s, csem_r, ysem_s, ysem_r, zsem_s, zsem_r, rsem_s, rsem_r, wsem,
):
    bl, rows, C, W = x_ref.shape
    cols, _, rows2, L = csend.shape
    modes = wbuf.shape[2]
    K2 = first_ref.shape[0]
    tiles = L // LANES
    slots = wbuf.shape[0]
    group = 2 * nb * bl
    tail = C - LANES
    me = lax.axis_index("ma")
    mine = lax.axis_index("ba")

    def weights(q):
        s = q % slots
        return [
            pltpu.make_async_copy(ref.at[:, q], wbuf.at[s, p], wsem.at[s, p])
            for p, ref in enumerate((wr_ref, wi_ref))
        ]

    for q in range(min(slots, cols)):
        for copy in weights(q):
            copy.start()

    barrier = pltpu.get_barrier_semaphore()
    for j in range(1, n):
        pl.semaphore_signal(
            barrier, inc=1, device_id={"ma": lax.rem(me + j, n)}, device_id_type=MESH
        )
    for j in range(1, nb):
        pl.semaphore_signal(
            barrier, inc=1, device_id={"ba": lax.rem(mine + j, nb)}, device_id_type=MESH
        )

    def over_ma(src, dst, s, r, q, j):
        to = lax.rem(me + j, n)
        return pltpu.make_async_remote_copy(
            src_ref=src.at[q, to], dst_ref=dst.at[q, me], send_sem=s.at[q, j],
            recv_sem=r.at[q, j], device_id={"ma": to}, device_id_type=MESH,
        )

    def over_ba(src, dst, s, r, q, j):
        to = lax.rem(mine + j, nb)
        return pltpu.make_async_remote_copy(
            src_ref=src.at[q, to], dst_ref=dst.at[q, mine], send_sem=s.at[q, j],
            recv_sem=r.at[q, j], device_id={"ba": to}, device_id_type=MESH,
        )

    order = sorted(range(1, n), key=lambda j: -min(j, n - j))

    @pl.loop(0, rows)
    def _(h):
        both = dot(first_ref[...], x_ref[:, h].reshape(L, W), (1, 1))
        for l in range(tiles):
            colf[l, pl.ds(pl.multiple_of(h * K2, K2), K2), :] = both[:, l * LANES:(l + 1) * LANES]

    sent = []
    for q in range(cols):
        @pl.loop(0, n)
        def _(d, q=q):
            for part in range(2):
                for l in range(tiles):
                    k = q * 2 * n + 2 * d + part
                    v = colf[l, pl.ds(k, rows, stride=K2), :]
                    csend[q, d, part * rows:(part + 1) * rows, l * LANES:(l + 1) * LANES] = v.astype(BF)

        crecv[q, me] = csend[q, me]
        if q == 0:
            pl.semaphore_wait(barrier, n - 1 + nb - 1)
        for j in order:
            c = over_ma(csend, crecv, csem_s, csem_r, q, j)
            c.start()
            sent.append(c)

    ysent, zsent = {}, {}

    def rows_down(q):
        for j in order:
            over_ma(csend, crecv, csem_s, csem_r, q, j).wait_recv()
        col = crecv[q].reshape(n * rows2, L)
        spec = dot(down_ref[...], col).astype(BF)
        for y in range(nb):
            ysend[q, y] = spec[y * 2 * modes:(y + 1) * 2 * modes]
        for j in range(1, nb):
            c = over_ba(ysend, yrecv, ysem_s, ysem_r, q, j)
            c.start()
            sent.append(c)
        yrecv[q, mine] = ysend[q, mine]

    def mix(q):
        for j in range(1, nb):
            over_ba(ysend, yrecv, ysem_s, ysem_r, q, j).wait_recv()
        for y in range(nb):
            whole = yrecv[q, y].astype(F32)
            for part in range(2):
                for b in range(bl):
                    v = whole[part * modes:(part + 1) * modes, b * C:(b + 1) * C]
                    head = v[:, :LANES]
                    rest = jnp.concatenate([v[:, LANES:], jnp.zeros((modes, LANES - tail), F32)], axis=1)
                    r1 = ((part * nb + y) * bl + b) * modes
                    r2 = (((1 - part) * nb + y) * bl + b) * modes
                    m1[0, r1:r1 + modes, :] = head
                    m1[1, r1:r1 + modes, :] = rest
                    m2[0, r2:r2 + modes, :] = head if part == 0 else -head
                    m2[1, r2:r2 + modes, :] = rest if part == 0 else -rest
        for copy in weights(q):
            copy.wait()
        s = q % slots

        def one(i, carry):
            at = pl.ds(i, group, stride=modes)
            a1 = jnp.concatenate([m1[0, at, :], m1[1, at, :][:, :tail]], axis=1).astype(BF)
            a2 = jnp.concatenate([m2[0, at, :], m2[1, at, :][:, :tail]], axis=1).astype(BF)
            o = dot(a1, wbuf[s, 0, i]) + dot(a2, wbuf[s, 1, i])
            mo[0, at, :] = o[:, :LANES]
            mo[1, at, :] = jnp.concatenate([o[:, LANES:], jnp.zeros((group, LANES - tail), F32)], axis=1)
            return carry

        lax.fori_loop(0, modes, one, 0, unroll=UNROLL)
        if q + slots < cols:
            for copy in weights(q + slots):
                copy.start()
        for y in range(nb):
            parts = []
            for part in range(2):
                pieces = []
                for b in range(bl):
                    r = ((part * nb + y) * bl + b) * modes
                    pieces += [mo[0, r:r + modes, :], mo[1, r:r + modes, :][:, :tail]]
                parts.append(jnp.concatenate(pieces, axis=1))
            zsend[q, y] = jnp.concatenate(parts, axis=0).astype(BF)
        for j in range(1, nb):
            c = over_ba(zsend, zrecv, zsem_s, zsem_r, q, j)
            c.start()
            sent.append(c)
        zrecv[q, mine] = zsend[q, mine]

    def rows_up(q):
        for j in range(1, nb):
            over_ba(zsend, zrecv, zsem_s, zsem_r, q, j).wait_recv()
        row = dot(up_ref[...], zrecv[q].reshape(nb * 2 * modes, L))
        rsend[q] = row.astype(BF).reshape(n, rows2, L)
        for j in order:
            c = over_ma(rsend, out_ref, rsem_s, rsem_r, q, j)
            c.start()
            sent.append(c)
        out_ref[q, me] = rsend[q, me]

    for t in range(cols + 2):
        if t < cols:
            rows_down(t)
        if 0 <= t - 2 < cols:
            rows_up(t - 2)
        if 0 <= t - 1 < cols:
            mix(t - 1)
    for q in range(cols):
        for j in order:
            over_ma(rsend, out_ref, rsem_s, rsem_r, q, j).wait_recv()
    for c in sent:
        c.wait_send()


UNROLL = 4


def final_kernel(rr_ref, x_ref, last_ref, skip_ref, bias_ref, out_ref, rf, turned, biases):
    bl, step, C, W = x_ref.shape
    cols, n, rows2, L = rr_ref.shape
    rows = rows2 // 2
    K2 = cols * n * 2
    tiles = L // LANES
    g = pl.program_id(0)

    @pl.when(g == 0)
    def _():
        turned[...] = skip_ref[...].astype(F32).T.astype(BF)
        wide = jnp.broadcast_to(bias_ref[...], (LANES, C)).T
        for l in range(W // LANES):
            biases[:, l * LANES:(l + 1) * LANES] = wide
        for q in range(cols):
            @pl.loop(0, n)
            def _(d, q=q):
                v = rr_ref[q, d].astype(F32)
                at = pl.ds(pl.multiple_of((q * n + d) * rows2, rows2), rows2)
                for l in range(tiles):
                    rf[l, at, :] = v[:, l * LANES:(l + 1) * LANES]

    for u in range(step):
        h = g * step + u
        r = jnp.concatenate([rf[l, pl.ds(h, K2, stride=rows), :] for l in range(tiles)], axis=1).astype(BF)
        spectral = dot(r, last_ref[...], (0, 0))
        for b in range(bl):
            v = spectral[b * C:(b + 1) * C] + dot(turned[...], x_ref[b, u]) + biases[...]
            inner = math.sqrt(2.0 / math.pi) * (v + 0.044715 * (v * v * v))
            out_ref[b, u] = (0.5 * v * (1.0 + jnp.tanh(inner))).astype(BF)


def kernels(n, nb, H, KX, KY, fields, weight_real, weight_imag, skip_weight, out_bias):
    bl, rows, W, C = fields.shape
    modes, cols = weight_real.shape[:2]
    L, K2 = bl * C, 2 * KY
    first, down, up, last = packed_tables(H, W, KX, KY, n, nb)
    fields = fields.transpose(0, 1, 3, 2)
    vmem = pl.BlockSpec(memory_space=pltpu.VMEM)
    hbm = pl.BlockSpec(memory_space=pl.ANY)
    tiles = L // LANES
    group = 2 * nb * bl
    ma_block = pltpu.VMEM((cols, n, 2 * rows, L), BF)
    ba_block = pltpu.VMEM((cols, nb, 2 * modes, L), BF)
    mix_block = pltpu.VMEM((2, group * modes, LANES), F32)
    dma = pltpu.SemaphoreType.DMA
    rr = pl.pallas_call(
        functools.partial(spectral_kernel, n, nb),
        out_shape=jax.ShapeDtypeStruct((cols, n, 2 * rows, L), BF),
        in_specs=[vmem, hbm, hbm, vmem, vmem, vmem],
        out_specs=vmem,
        scratch_shapes=[
            pltpu.VMEM((tiles, rows * K2, LANES), F32), ma_block, ma_block, ba_block, ba_block,
            mix_block, mix_block, mix_block, ba_block, ba_block, ma_block,
            pltpu.VMEM((min(2, cols), 2, modes, C, C), BF),
            dma((cols, n)), dma((cols, n)), dma((cols, nb)), dma((cols, nb)), dma((cols, nb)),
            dma((cols, nb)), dma((cols, n)), dma((cols, n)), dma((min(2, cols), 2)),
        ],
        compiler_params=pltpu.CompilerParams(
            collective_id=0, has_side_effects=True, vmem_limit_bytes=VMEM_LIMIT
        ),
        name="spectral",
    )(fields, weight_real, weight_imag, first, down, up)
    step = 2 if rows % 2 == 0 else 1
    slab = pl.BlockSpec((bl, step, C, W), lambda g: (0, g, 0, 0))
    out = pl.pallas_call(
        final_kernel,
        grid=(rows // step,),
        out_shape=jax.ShapeDtypeStruct(fields.shape, BF),
        in_specs=[vmem, slab, vmem, vmem, vmem],
        out_specs=slab,
        scratch_shapes=[
            pltpu.VMEM((tiles, K2 * rows, LANES), F32), pltpu.VMEM((C, C), BF), pltpu.VMEM((C, W), F32)
        ],
        compiler_params=pltpu.CompilerParams(vmem_limit_bytes=VMEM_LIMIT),
        name="finish",
    )(rr, fields, last, skip_weight, out_bias.reshape(1, C))
    return out.transpose(0, 1, 3, 2)


def fits(n, nb, fields, weights):
    bl, rows, W, C = fields.shape
    modes, cols = weights.shape[:2]
    whole = 2 * modes * cols * C * 256 * 2
    return (
        rows % 16 == 0 and modes % 8 == 0 and (bl * C) % LANES == 0 and LANES < C < 2 * LANES
        and 2 * nb * bl == 8 and W % LANES == 0 and whole * min(2, cols) // cols < 36 * 2**20
        and cols * n * 2 % LANES == 0
    )


def any_size(n, nb, H, KX, KY, fields, weight_real, weight_imag, skip_weight, out_bias):
    bl, rows, W, C = fields.shape
    modes, cols = weight_real.shape[:2]
    first, down, up, last = packed_tables(H, W, KX, KY, n, nb)
    col = jnp.einsum("qdpw,brwc->dqprbc", first.reshape(cols, n, 2, W), fields, preferred_element_type=F32)
    col = lax.all_to_all(col.astype(BF), "ma", split_axis=0, concat_axis=0, tiled=True)
    spec = jnp.einsum("ypidrh,dqrhbc->ypqbic", down.reshape(nb, 2, modes, n, 2, rows), col, preferred_element_type=F32)
    spec = lax.all_to_all(spec.astype(BF), "ba", split_axis=0, concat_axis=0, tiled=True)
    re, im = spec[:, 0], spec[:, 1]
    mul = functools.partial(jnp.einsum, "yqbic,iqco->yqbio", preferred_element_type=F32)
    mixed = jnp.stack([
        mul(re, weight_real) - mul(im, weight_imag), mul(re, weight_imag) + mul(im, weight_real)
    ], 1)
    mixed = lax.all_to_all(mixed.astype(BF), "ba", split_axis=0, concat_axis=0, tiled=True)
    row = jnp.einsum("drhypi,ypqbic->dqrhbc", up.reshape(n, 2, rows, nb, 2, modes), mixed, preferred_element_type=F32)
    row = lax.all_to_all(row.astype(BF), "ma", split_axis=0, concat_axis=0, tiled=True)
    spectral = jnp.einsum("qdrw,dqrhbc->bhwc", last.reshape(cols, n, 2, W), row, preferred_element_type=F32)
    skip = jnp.dot(fields.reshape(-1, C), skip_weight, preferred_element_type=F32).reshape(spectral.shape)
    return jax.nn.gelu(spectral + skip + out_bias).astype(BF)


def solution(mesh):
    n, nb = mesh.shape["ma"], mesh.shape["ba"]

    def local(fields, weight_real, weight_imag, skip_weight, out_bias):
        sizes = (fields.shape[1] * n, weight_real.shape[0] * nb, weight_real.shape[1] * n)
        run = kernels if fits(n, nb, fields, weight_real) else any_size
        return run(n, nb, *sizes, fields, weight_real, weight_imag, skip_weight, out_bias)

    split = P("ba", "ma", None, None)
    return jax.shard_map(
        local, mesh=mesh, in_specs=(split, split, split, P(), P()), out_specs=split, check_vma=False
    )
```

profile of v0, /device:TPU:1, one launch (start us, length us, event | category | flops | bytes accessed | tf_op | source)
XLA Modules:
  0.0 94.9 jit_solution(14695200886748015237)
XLA Ops:
  0.0 0.0 copy-start
  0.0 0.0 copy-start.7
  0.0 1.7 %fusion.19 = bf16[64,1,2,4,2,192]{5,0,3,4,2,1:T(8,128)(2,1)S(1)} fusion(bf16[64,2,256,1,1]{2,0,4,3,1:T(8,128)(2,1)} %constant.31, bf16[2,4,256,192]{2,3,1,0:T(8,128)(2,1)} %param.9), kind=kOutput, calls=%fused_computation.23 | convolution fusion | flops 100859904 | bytes 1245184 | tf_op jit(solution)/shard_map/qdpw,brwc->dqprbc/dot_general | solution.py:312
  1.7 0.4 copy.20
  2.1 32.5 %all_to_all.20 = bf16[64,1,2,4,2,192]{5,3,4,2,1,0:T(4,128)(2,1)S(1)} all-to-all(bf16[64,1,2,4,2,192]{5,3,4,2,1,0:T(4,128)(2,1)S(1)} %copy.20), channel_id=1, replica_groups=mesh['ma'=64,'ba'=8] {'ma'}, dimensions={0} | all-to-all | bytes 786432 | tf_op jit(solution)/shard_map/all_to_all | solution.py:313
  34.7 0.0 copy-done.7
  34.7 0.5 fusion.21
  35.2 0.2 copy.22
  35.4 16.6 %all_to_all.21 = bf16[8,2,1,2,14,192]{5,3,4,2,1,0:T(2,128)(2,1)S(1)} all-to-all(bf16[8,2,1,2,14,192]{5,3,4,2,1,0:T(2,128)(2,1)S(1)} %copy.22), channel_id=1, replica_groups=mesh['ma'=64,'ba'=8] {'ba'}, dimensions={0} | all-to-all | bytes 344064 | tf_op jit(solution)/shard_map/all_to_all | solution.py:315
  52.0 0.2 fusion.50
  52.2 0.0 copy-done
  52.2 0.0 copy-start.1
  52.2 0.3 fusion.11
  52.5 0.3 fusion.9
  52.8 0.7 copy-done.1
  53.6 0.3 fusion.34
  53.8 0.0 copy-start.3
  53.9 0.3 fusion.37
  54.2 0.2 copy.25
  54.4 10.9 %all_to_all.22 = bf16[8,2,1,2,14,192]{5,3,4,2,1,0:T(2,128)(2,1)S(1)} all-to-all(bf16[8,2,1,2,14,192]{5,3,4,2,1,0:T(2,128)(2,1)S(1)} %copy.25), channel_id=1, replica_groups=mesh['ma'=64,'ba'=8] {'ba'}, dimensions={0} | all-to-all | bytes 344064 | tf_op jit(solution)/shard_map/all_to_all | solution.py:321
  65.3 0.0 copy-done.3
  65.3 0.0 copy-start.4
  65.3 0.3 fusion.18
  65.7 0.4 copy.27
  66.1 0.0 copy-start.2
  66.1 0.0 copy-start.5
  66.1 0.0 copy-start.6
  66.1 26.5 %all_to_all.23 = bf16[64,1,2,4,2,192]{5,3,2,4,1,0:T(4,128)(2,1)S(1)} all-to-all(bf16[64,1,2,4,2,192]{5,3,2,4,1,0:T(4,128)(2,1)S(1)} %copy.27), channel_id=1, replica_groups=mesh['ma'=64,'ba'=8] {'ma'}, dimensions={0} | all-to-all | bytes 786432 | tf_op jit(solution)/shard_map/all_to_all | solution.py:323
  92.6 0.0 copy-done.4
  92.6 0.5 fusion.43
  93.1 0.0 copy-done.2
  93.1 0.0 copy-done.5
  93.1 0.0 copy-done.6
  93.1 0.8 fusion.7
  93.9 0.9 copy.31
  (1 shorter events, 0.0 us)
Async XLA Ops:
  0.0 52.2 %copy-start = (bf16[14,1,192,192]{3,2,1,0:T(8,128)(2,1)S(1)}, bf16[14,1,192,192]{3,2,1,0:T(8,128)(2,1)}, u32[]{:S(2)}) copy-start(bf16[14,1,192,192]{3,2,1,0:T(8,128)(2,1)} %param.10) | copy-start | bytes 3096580
  0.0 34.7 %copy-start.7 = (bf16[8,2,14,64,2,4,1]{3,2,4,5,1,0,6:T(8,128)(2,1)S(1)}, bf16[8,2,14,64,2,4,1]{3,2,4,5,1,0,6:T(8,128)(2,1)}, u32[]{:S(2)}) copy-start(bf16[8,2,14,64,2,4,1]{3,2,4,5,1,0,6:T(8,128)(2,1)} %constant.32) | copy-start | bytes 688132
  52.2 1.3 %copy-start.1 = (bf16[14,1,192,192]{3,2,1,0:T(8,128)(2,1)S(1)}, bf16[14,1,192,192]{3,2,1,0:T(8,128)(2,1)}, u32[]{:S(2)}) copy-start(bf16[14,1,192,192]{3,2,1,0:T(8,128)(2,1)} %param.11) | copy-start | bytes 3096580
  53.8 11.5 %copy-start.3 = (bf16[64,2,4,8,2,14,1]{0,5,3,4,2,1,6:T(8,128)(2,1)S(1)}, bf16[64,2,4,8,2,14,1]{0,5,3,4,2,1,6:T(8,128)(2,1)}, u32[]{:S(2)}) copy-start(bf16[64,2,4,8,2,14,1]{0,5,3,4,2,1,6:T(8,128)(2,1)} %constant.33) | copy-start | bytes 688132
  65.3 27.3 %copy-start.4 = (bf16[64,2,256,1,1]{2,0,1,4,3:T(8,128)(2,1)S(1)}, bf16[64,2,256,1,1]{2,0,1,4,3:T(8,128)(2,1)}, u32[]{:S(2)}) copy-start(bf16[64,2,256,1,1]{2,0,1,4,3:T(8,128)(2,1)} %constant.34) | copy-start | bytes 196612
  66.1 27.0 %copy-start.2 = (bf16[2,4,256,192]{2,3,1,0:T(8,128)(2,1)S(1)}, bf16[2,4,256,192]{2,3,1,0:T(8,128)(2,1)}, u32[]{:S(2)}) copy-start(bf16[2,4,256,192]{2,3,1,0:T(8,128)(2,1)} %param.9) | copy-start | bytes 2359300
  66.1 27.0 %copy-start.5 = (bf16[192,192]{1,0:T(8,128)(2,1)S(1)}, bf16[192,192]{1,0:T(8,128)(2,1)}, u32[]{:S(2)}) copy-start(bf16[192,192]{1,0:T(8,128)(2,1)} %param.12) | copy-start | bytes 221188
  66.1 27.0 %copy-start.6 = (f32[192]{0:T(256)S(1)}, f32[192]{0:T(256)}, u32[]{:S(2)}) copy-start(f32[192]{0:T(256)} %param.13) | copy-start | bytes 2308
where the time goes:
time: 95.2 us; the launch traced here: 94.9 us
  blocking collectives  86.5 us (91%)
  matrix products  5.02 us (5%)
  local copies, waits for them, and re-layouts  3.11 us (3%)
    all_to_all x1, blocking collectives, any_size(): lax.all_to_all(col.astype(BF), 'ma', split_axis=0, concat_axis=0, tiled=T...  32.5 us
    all_to_all x1, blocking collectives, any_size(): lax.all_to_all(row.astype(BF), 'ma', split_axis=0, concat_axis=0, tiled=T...  26.5 us
    all_to_all x1, blocking collectives, any_size(): lax.all_to_all(spec.astype(BF), 'ba', split_axis=0, concat_axis=0, tiled=...  16.6 us
    all_to_all x1, blocking collectives, any_size(): lax.all_to_all(mixed.astype(BF), 'ba', split_axis=0, concat_axis=0, tiled...  10.9 us

commit v1 on v0

v1 whole, which is shorter than its diff:
```python
import functools
import math

import jax
import jax.numpy as jnp
import numpy as np
from jax import lax
from jax.experimental import pallas as pl
from jax.experimental.pallas import tpu as pltpu
from jax.sharding import PartitionSpec as P

MESH = pl.DeviceIdType.MESH
BF = jnp.bfloat16
F32 = jnp.float32
LANES = 128
PAD = 32
GRID = (8, 4, 2)
FAR = (4, 3, 5, 2, 6, 1, 7, 0)


def angles(left, right, extent):
    turn = 2.0 * np.pi / extent * ((left[:, None] * right[None, :]) % extent)
    return np.cos(turn), np.sin(turn)


def packed_tables(H, W, KX, KY, n, nb):
    rows, modes = H // n, KX // nb
    s = 1.0 / math.sqrt(H * W)
    ky = np.arange(KY)
    eye = np.eye(rows)
    cos_w, sin_w = angles(ky, np.arange(W), W)
    g = np.where(ky == 0, 1.0, 2.0)[:, None] * s
    wide = []
    for f in (s, g):
        both = np.stack([cos_w * f, -sin_w * f], 1)
        wide.append(np.einsum("kpw,hg->khpgw", both, eye).reshape(KY * rows * 2, rows * W))
    i = np.arange(KX)
    kx = np.where(i < KX // 2, i, i + H - KX)
    cos_h, sin_h = angles(kx, np.arange(H), H)
    cos_h, sin_h = cos_h.reshape(nb, modes, H), sin_h.reshape(nb, modes, H)
    down = np.zeros((nb, PAD, H, 2))
    down[:, :modes, :, 0], down[:, :modes, :, 1] = cos_h, sin_h
    down[:, modes:2 * modes, :, 0], down[:, modes:2 * modes, :, 1] = -sin_h, cos_h
    up = np.zeros((H, 2, nb, PAD))
    ct, st = cos_h.transpose(2, 0, 1), sin_h.transpose(2, 0, 1)
    up[:, 0, :, :modes], up[:, 0, :, modes:2 * modes] = ct, -st
    up[:, 1, :, :modes], up[:, 1, :, modes:2 * modes] = st, ct
    tables = (wide[0], down.reshape(nb * PAD, 2 * H), up.reshape(2 * H, nb * PAD), wide[1])
    return [jnp.asarray(a.astype(np.float32)).astype(BF) for a in tables]


def dot(a, b, over=(1, 0)):
    return lax.dot_general(a, b, (((over[0],), (over[1],)), ((), ())), preferred_element_type=F32)


def fold(a, tail):
    b0, b1 = a
    return [b0[:LANES], jnp.concatenate([b0[LANES:], b1[LANES:]], axis=0), b1[:LANES]]


def spectral_kernel(
    n, nb, groups, x_ref, wr_ref, wi_ref, skip_ref, bias_ref, first_ref, down_ref, up_ref, last_ref,
    rr_ref, sk_ref, lv_ref,
    xv, fv, dv, uv, wv, sv, csend, crecv, ysend, yrecv, m1, mo, zsend, zrecv, rsend,
    lsem, csem_s, csem_r, ysem_s, ysem_r, zsem_s, zsem_r, rsem_s, rsem_r,
):
    bl, rows, C, W = x_ref.shape
    modes = wr_ref.shape[0]
    tiles = len(groups) and groups[-1][1]
    tail = C - LANES
    used = 2 * modes
    me = lax.axis_index("ma")
    mine = lax.axis_index("ba")
    az, ax, ac = me // 8, (me // 2) % 4, me % 2

    loads = [
        pltpu.make_async_copy(a, b, lsem.at[k]) for k, (a, b) in enumerate((
            (x_ref, xv), (first_ref, fv), (down_ref, dv), (skip_ref, sv),
            (wr_ref.at[:, 0], wv.at[0]), (wi_ref.at[:, 0], wv.at[1]), (up_ref, uv), (last_ref, lv_ref),
        ))
    ]
    for c in loads:
        c.start()

    def peer(dz, r):
        return (az + dz) % 8 * 8 + (ax + r // 2) % 4 * 2 + (ac + r) % 2

    def each_ma(body):
        for dz in FAR:
            @pl.loop(1 if dz == 0 else 0, 8)
            def _(r, dz=dz):
                body(dz * 8 + r, peer(dz, r))

    barrier = pltpu.get_barrier_semaphore()

    @functools.partial(each_ma)
    def _(j, to):
        pl.semaphore_signal(barrier, inc=1, device_id={"ma": to}, device_id_type=MESH)

    @pl.loop(1, nb)
    def _(j):
        pl.semaphore_signal(barrier, inc=1, device_id={"ba": (mine + j) % nb}, device_id_type=MESH)

    zrecv[:, :, used:, :] = jnp.zeros((tiles, nb, PAD - used, LANES), BF)

    def over_ma(src, dst, s, r, q, j, to):
        a, b = groups[q]
        return pltpu.make_async_remote_copy(
            src_ref=src.at[a:b, to], dst_ref=dst.at[a:b, me], send_sem=s.at[q, j],
            recv_sem=r.at[q, j], device_id={"ma": to}, device_id_type=MESH,
        )

    def over_ba(src, dst, s, r, q, j):
        a, b = groups[q]
        to = (mine + j) % nb
        return pltpu.make_async_remote_copy(
            src_ref=src.at[a:b, to, 0:used], dst_ref=dst.at[a:b, mine, 0:used], send_sem=s.at[q, j],
            recv_sem=r.at[q, j], device_id={"ba": to}, device_id_type=MESH,
        )

    def ma_all(what, *refs):
        def go(q):
            each_ma(lambda j, to: getattr(over_ma(*refs, q, j, to), what)())
        return go

    def ba_all(what, *refs):
        def go(q):
            @pl.loop(1, nb)
            def _(j):
                getattr(over_ba(*refs, q, j), what)()
        return go

    cols = (csend, crecv, csem_s, csem_r)
    specs = (ysend, yrecv, ysem_s, ysem_r)
    mixed = (zsend, zrecv, zsem_s, zsem_r)
    lines = (rsend, rr_ref, rsem_s, rsem_r)

    loads[0].wait()
    loads[1].wait()
    x = [
        jnp.concatenate([xv[b, h] for h in range(rows)], axis=1) for b in range(bl)
    ]
    xt = fold(x, tail)
    both = dot(fv[...], jnp.concatenate(xt, axis=0), (1, 1))
    for t in range(tiles):
        csend[t] = both[:, t * LANES:(t + 1) * LANES].astype(BF).reshape(n, 2 * rows, LANES)
    pl.semaphore_wait(barrier, n - 1 + nb - 1)
    for q, (a, b) in enumerate(groups):
        ma_all("start", *cols)(q)
    crecv[:, me] = csend[:, me]

    loads[3].wait()
    turned = sv[...].astype(F32).T.astype(BF)
    wide = jnp.broadcast_to(bias_ref[...], (LANES, C)).T
    bias = jnp.concatenate([wide, wide], axis=1)
    for h in range(rows):
        sk = [dot(turned, xv[b, h]) + bias for b in range(bl)]
        for t, v in enumerate(fold(sk, tail)):
            sk_ref[t, :, h * W:(h + 1) * W] = v

    loads[2].wait()
    for q, (a, b) in enumerate(groups):
        ma_all("wait_recv", *cols)(q)
        col = jnp.concatenate([crecv[t].reshape(n * 2 * rows, LANES) for t in range(a, b)], axis=1)
        spec = dot(dv[...], col).astype(BF)
        for t in range(a, b):
            ysend[t] = spec[:, (t - a) * LANES:(t - a + 1) * LANES].reshape(nb, PAD, LANES)
        ba_all("start", *specs)(q)
        yrecv[a:b, mine] = ysend[a:b, mine]

    for q, (a, b) in enumerate(groups):
        ba_all("wait_recv", *specs)(q)
    for t in range(tiles):
        m1[t] = yrecv[t].reshape(nb * PAD, LANES).astype(F32)
    loads[4].wait()
    loads[5].wait()
    for i in range(modes):
        parts = []
        for p in range(2):
            r = [m1[t, pl.ds(p * modes + i, nb, stride=PAD), :] for t in range(tiles)]
            parts.append([
                jnp.concatenate([r[0], r[1][:, :tail]], axis=1),
                jnp.concatenate([r[2], r[1][:, tail:]], axis=1),
            ])
        re, im = parts
        a1 = jnp.concatenate([re[0], im[0], re[1], im[1]], axis=0).astype(BF)
        a2 = jnp.concatenate([-im[0], re[0], -im[1], re[1]], axis=0).astype(BF)
        o = dot(a1, wv[0, i]) + dot(a2, wv[1, i])
        for p in range(2):
            b0, b1 = o[p * nb:(p + 1) * nb], o[(2 + p) * nb:(3 + p) * nb]
            at = pl.ds(p * modes + i, nb, stride=PAD)
            mo[0, at, :] = b0[:, :LANES]
            mo[1, at, :] = jnp.concatenate([b0[:, LANES:], b1[:, LANES:]], axis=1)
            mo[2, at, :] = b1[:, :LANES]
    for t in range(tiles):
        zsend[t] = mo[t].astype(BF).reshape(nb, PAD, LANES)
    for q, (a, b) in enumerate(groups):
        ba_all("start", *mixed)(q)
    zrecv[:, mine, 0:used] = zsend[:, mine, 0:used]

    loads[6].wait()
    for q, (a, b) in enumerate(groups):
        ba_all("wait_recv", *mixed)(q)
        z = jnp.concatenate([zrecv[t].reshape(nb * PAD, LANES) for t in range(a, b)], axis=1)
        row = dot(uv[...], z).astype(BF)
        for t in range(a, b):
            rsend[t] = row[:, (t - a) * LANES:(t - a + 1) * LANES].reshape(n, 2 * rows, LANES)
        ma_all("start", *lines)(q)
        rr_ref[a:b, me] = rsend[a:b, me]

    loads[7].wait()
    for q in range(len(groups)):
        ma_all("wait_send", *cols)(q)
        ba_all("wait_send", *specs)(q)
        ba_all("wait_send", *mixed)(q)
    for q in range(len(groups)):
        ma_all("wait_recv", *lines)(q)
    for q in range(len(groups)):
        ma_all("wait_send", *lines)(q)


def final_kernel(rr_ref, sk_ref, lv_ref, out_ref, ov, sems):
    bl, rows, C, W = out_ref.shape
    tiles, n = rr_ref.shape[:2]
    tail = C - LANES
    r = jnp.concatenate([rr_ref[t].reshape(-1, LANES) for t in range(tiles)], axis=1)
    rt = r.astype(F32).T.astype(BF)
    copies = []
    for h in range(rows):
        at = slice(h * W, (h + 1) * W)
        spectral = dot(rt, lv_ref[:, at])
        for t in range(tiles):
            v = spectral[t * LANES:(t + 1) * LANES] + sk_ref[t, :, at]
            inner = math.sqrt(2.0 / math.pi) * (v + 0.044715 * (v * v * v))
            o = (0.5 * v * (1.0 + jnp.tanh(inner))).astype(BF)
            if t == 1:
                ov[0, h, LANES:] = o[:tail]
                ov[1, h, LANES:] = o[tail:]
            else:
                ov[t // 2, h, :LANES] = o
        c = pltpu.make_async_copy(ov.at[:, h], out_ref.at[:, h], sems.at[h])
        c.start()
        copies.append(c)
    for c in copies:
        c.wait()


GROUPS = ((0, 3),)


def kernels(n, nb, H, KX, KY, fields, weight_real, weight_imag, skip_weight, out_bias):
    bl, rows, W, C = fields.shape
    modes = weight_real.shape[0]
    first, down, up, last = packed_tables(H, W, KX, KY, n, nb)
    fields = fields.transpose(0, 1, 3, 2)
    vmem = pl.BlockSpec(memory_space=pltpu.VMEM)
    hbm = pl.BlockSpec(memory_space=pl.ANY)
    tiles = bl * C // LANES
    ma_block = pltpu.VMEM((tiles, n, 2 * rows, LANES), BF)
    ba_block = pltpu.VMEM((tiles, nb, PAD, LANES), BF)
    mix_block = pltpu.VMEM((tiles, nb * PAD, LANES), F32)
    dma = pltpu.SemaphoreType.DMA
    ng = len(GROUPS)
    rr, sk, lv = pl.pallas_call(
        functools.partial(spectral_kernel, n, nb, GROUPS),
        out_shape=(
            jax.ShapeDtypeStruct((tiles, n, 2 * rows, LANES), BF),
            jax.ShapeDtypeStruct((tiles, LANES, rows * W), F32),
            jax.ShapeDtypeStruct(last.shape, BF),
        ),
        in_specs=[hbm, hbm, hbm, hbm, vmem, hbm, hbm, hbm, hbm],
        out_specs=(vmem, vmem, vmem),
        scratch_shapes=[
            pltpu.VMEM(fields.shape, BF), pltpu.VMEM(first.shape, BF), pltpu.VMEM(down.shape, BF),
            pltpu.VMEM(up.shape, BF), pltpu.VMEM((2, modes, C, C), BF), pltpu.VMEM((C, C), BF),
            ma_block, ma_block, ba_block, ba_block, mix_block, mix_block, ba_block, ba_block, ma_block,
            dma((8,)), dma((ng, n)), dma((ng, n)), dma((ng, nb)), dma((ng, nb)), dma((ng, nb)),
            dma((ng, nb)), dma((ng, n)), dma((ng, n)),
        ],
        compiler_params=pltpu.CompilerParams(
            collective_id=0, has_side_effects=True, vmem_limit_bytes=48 * 2**20
        ),
        name="spectral",
    )(fields, weight_real, weight_imag, skip_weight, out_bias.reshape(1, C), first, down, up, last)
    out = pl.pallas_call(
        final_kernel,
        out_shape=jax.ShapeDtypeStruct(fields.shape, BF),
        in_specs=[vmem, vmem, vmem],
        out_specs=hbm,
        scratch_shapes=[pltpu.VMEM(fields.shape, BF), dma((rows,))],
        compiler_params=pltpu.CompilerParams(vmem_limit_bytes=16 * 2**20),
        name="finish",
    )(rr, sk, lv)
    return out.transpose(0, 1, 3, 2)


def solution(mesh):
    n, nb = mesh.shape["ma"], mesh.shape["ba"]

    def local(fields, weight_real, weight_imag, skip_weight, out_bias):
        sizes = (fields.shape[1] * n, weight_real.shape[0] * nb, weight_real.shape[1] * n)
        return kernels(n, nb, *sizes, fields, weight_real, weight_imag, skip_weight, out_bias)

    split = P("ba", "ma", None, None)
    return jax.shard_map(
        local, mesh=mesh, in_specs=(split, split, split, P(), P()), out_specs=split, check_vma=False
    )
```

time: 95.2 us -> 70.4 us (0.74)
  blocking collectives: 86.5 us -> 0 us
  Pallas kernels: 0 us -> 61.6 us
  local copies, waits for them, and re-layouts: 3.11 us -> 8.45 us
  matrix products: 5.02 us -> 0 us
    all_to_all x4 -> x0, blocking collectives: 86.5 us -> none  [the longest x1 32.5 us: any_size(): lax.all_to_all(col.astype(BF), 'ma', split_axis=0, concat_axis=0, tiled=T...]
    pallas_call x0 -> x2, Pallas kernels: none -> 61.6 us  [the longest x1 59.8 us: kernels(): pl.pallas_call(functools.partial(spectral_kernel, n, nb, GROUPS), out_sha...]
    unnamed x16, local copies, waits for them, and re-layouts: 0.78 us -> 8.45 us
    dot_general x9 -> x0, matrix products: 5.02 us -> none  [the longest x1 1.7 us: any_size(): jnp.einsum('qdpw,brwc->dqprbc', first.reshape(cols, n, 2, W), fields, pre...]
    convert_element_type x4 -> x0, local copies, waits for them, and re-layouts: 1.99 us -> none  [the longest x1 0.93 us: any_size(): return jax.nn.gelu(spectral + skip + out_bias).astype(BF)]
where the time goes in v1:
time: 70.4 us; the launch traced here: 70.1 us
  Pallas kernels  61.6 us (88%)
  local copies, waits for them, and re-layouts  8.45 us (12%)
    pallas_call x1, Pallas kernels, kernels(): pl.pallas_call(functools.partial(spectral_kernel, n, nb, GROUPS), out_sha...  59.8 us
    unnamed x16, local copies, waits for them, and re-layouts  8.45 us
    pallas_call x1, Pallas kernels, kernels(): pl.pallas_call(final_kernel, out_shape=jax.ShapeDtypeStruct(fields.shape,...  1.74 us

profile of v1, /device:TPU:1, one launch (start us, length us, event | category | flops | bytes accessed | tf_op | source)
XLA Modules:
  0.0 70.1 jit_solution(68453986662170083)
XLA Ops:
  0.0 0.0 copy-start.1
  0.0 1.2 %copy-done.1 = bf16[512,1024]{1,0:T(8,128)(2,1)S(1)} copy-done((bf16[512,1024]{1,0:T(8,128)(2,1)S(1)}, bf16[512,1024]{1,0:T(8,128)(2,1)}, u32[]{:S(2)}) %copy-start.1) | copy-done | bytes 1048600
  1.2 0.0 copy-start.2
  1.2 1.2 %copy-done.2 = bf16[512,1024]{1,0:T(8,128)(2,1)S(1)} copy-done((bf16[512,1024]{1,0:T(8,128)(2,1)S(1)}, bf16[512,1024]{1,0:T(8,128)(2,1)}, u32[]{:S(2)}) %copy-start.2) | copy-done | bytes 1048600
  2.5 0.0 copy-start.3
  2.5 1.1 %copy-done.3 = bf16[2,4,256,192]{2,3,1,0:T(8,128)(2,1)S(1)} copy-done((bf16[2,4,256,192]{2,3,1,0:T(8,128)(2,1)S(1)}, bf16[2,4,256,192]{2,3,1,0:T(8,128)(2,1)}, u32[]{:S(2)}) %copy-start.3) | copy-done | bytes 786456
  3.6 0.0 copy-start.4
  3.6 0.9 %copy-done.4 = bf16[512,256]{1,0:T(8,128)(2,1)S(1)} copy-done((bf16[512,256]{1,0:T(8,128)(2,1)S(1)}, bf16[512,256]{1,0:T(8,128)(2,1)}, u32[]{:S(2)}) %copy-start.4) | copy-done | bytes 262168
  4.5 0.0 copy-start.5
  4.5 0.9 %copy-done.5 = bf16[256,512]{1,0:T(8,128)(2,1)S(1)} copy-done((bf16[256,512]{1,0:T(8,128)(2,1)S(1)}, bf16[256,512]{1,0:T(8,128)(2,1)}, u32[]{:S(2)}) %copy-start.5) | copy-done | bytes 262168
  5.5 0.0 copy-start.6
  5.5 0.9 %copy-done.6 = bf16[192,192]{1,0:T(8,128)(2,1)S(1)} copy-done((bf16[192,192]{1,0:T(8,128)(2,1)S(1)}, bf16[192,192]{1,0:T(8,128)(2,1)}, u32[]{:S(2)}) %copy-start.6) | copy-done | bytes 73752
  6.4 0.0 copy-start.7
  6.4 0.7 copy-done.7
  7.1 59.8 %spectral.1 = (bf16[3,64,8,128]{3,2,1,0:T(8,128)(2,1)S(1)}, f32[3,128,1024]{2,1,0:T(8,128)}, bf16[512,1024]{1,0:T(8,128)(2,1)S(1)}) custom-call(bf16[2,4,192,256]{3,2,1,0:T(8,128)(2,1)S(1)} %bitcast.3, bf16[14,1,192,192]{3,2,1,0:T(8,128)(2,1)} %wr_ref.1, bf16[14,1,192,192]{3,2,1,0:T(8,128)(2,1)} %wi_ref.1, bf16[192,192]{1,0:T(8,128)(2,1)S(1)} %copy-done.6, ...), custom_call_target="tpu_custom_call" | custom-call | tf_op jit(solution)/shard_map/spectral/pallas_call | solution.py:264
  66.9 0.0 copy-start
  66.9 1.4 %copy-done = f32[3,128,1024]{2,1,0:T(8,128)S(1)} copy-done((f32[3,128,1024]{2,1,0:T(8,128)S(1)}, f32[3,128,1024]{2,1,0:T(8,128)}, u32[]{:S(2)}) %copy-start) | copy-done | bytes 1572888
  68.3 1.7 %finish.1 = bf16[2,4,192,256]{3,2,1,0:T(8,128)(2,1)} custom-call(bf16[3,64,8,128]{3,2,1,0:T(8,128)(2,1)S(1)} %get-tuple-element.8.rr_ref, f32[3,128,1024]{2,1,0:T(8,128)S(1)} %copy-done, bf16[512,1024]{1,0:T(8,128)(2,1)S(1)} %get-tuple-element.10.lv_ref), custom_call_target="tpu_custom_call" | custom-call | tf_op jit(solution)/shard_map/finish/pallas_call | solution.py:285
Async XLA Ops:
  0.0 1.2 %copy-start.1 = (bf16[512,1024]{1,0:T(8,128)(2,1)S(1)}, bf16[512,1024]{1,0:T(8,128)(2,1)}, u32[]{:S(2)}) copy-start(bf16[512,1024]{1,0:T(8,128)(2,1)} %constant.18.last_ref) | copy-start | bytes 3145732
  1.2 1.2 %copy-start.2 = (bf16[512,1024]{1,0:T(8,128)(2,1)S(1)}, bf16[512,1024]{1,0:T(8,128)(2,1)}, u32[]{:S(2)}) copy-start(bf16[512,1024]{1,0:T(8,128)(2,1)} %constant.15.first_ref) | copy-start | bytes 3145732
  2.5 1.1 %copy-start.3 = (bf16[2,4,256,192]{2,3,1,0:T(8,128)(2,1)S(1)}, bf16[2,4,256,192]{2,3,1,0:T(8,128)(2,1)}, u32[]{:S(2)}) copy-start(bf16[2,4,256,192]{2,3,1,0:T(8,128)(2,1)} %param.9) | copy-start | bytes 2359300
  3.6 0.9 %copy-start.4 = (bf16[512,256]{1,0:T(8,128)(2,1)S(1)}, bf16[512,256]{1,0:T(8,128)(2,1)}, u32[]{:S(2)}) copy-start(bf16[512,256]{1,0:T(8,128)(2,1)} %constant.17.up_ref) | copy-start | bytes 786436
  4.5 0.9 %copy-start.5 = (bf16[256,512]{1,0:T(8,128)(2,1)S(1)}, bf16[256,512]{1,0:T(8,128)(2,1)}, u32[]{:S(2)}) copy-start(bf16[256,512]{1,0:T(8,128)(2,1)} %constant.16.down_ref) | copy-start | bytes 786436
  5.5 0.9 %copy-start.6 = (bf16[192,192]{1,0:T(8,128)(2,1)S(1)}, bf16[192,192]{1,0:T(8,128)(2,1)}, u32[]{:S(2)}) copy-start(bf16[192,192]{1,0:T(8,128)(2,1)} %skip_ref.1) | copy-start | bytes 221188
  6.4 0.7 copy-start.7
  66.9 1.4 %copy-start = (f32[3,128,1024]{2,1,0:T(8,128)S(1)}, f32[3,128,1024]{2,1,0:T(8,128)}, u32[]{:S(2)}) copy-start(f32[3,128,1024]{2,1,0:T(8,128)} %get-tuple-element.9.sk_ref) | copy-start | bytes 4718596

commit v2 on v1

--- a/solution.py
+++ b/solution.py
@@ -61,7 +61,7 @@
 def spectral_kernel(
     n, nb, groups, x_ref, wr_ref, wi_ref, skip_ref, bias_ref, first_ref, down_ref, up_ref, last_ref,
     rr_ref, sk_ref, lv_ref,
-    xv, fv, dv, uv, wv, sv, csend, crecv, ysend, yrecv, m1, mo, zsend, zrecv, rsend,
+    xv, fv, dv, uv, wv, sv, bv, csend, crecv, ysend, yrecv, m1, mo, zsend, zrecv, rsend,
     lsem, csem_s, csem_r, ysem_s, ysem_r, zsem_s, zsem_r, rsem_s, rsem_r,
 ):
     bl, rows, C, W = x_ref.shape
@@ -77,6 +77,7 @@
         pltpu.make_async_copy(a, b, lsem.at[k]) for k, (a, b) in enumerate((
             (x_ref, xv), (first_ref, fv), (down_ref, dv), (skip_ref, sv),
             (wr_ref.at[:, 0], wv.at[0]), (wi_ref.at[:, 0], wv.at[1]), (up_ref, uv), (last_ref, lv_ref),
+            (bias_ref, bv),
         ))
     ]
     for c in loads:
@@ -86,10 +87,14 @@
         return (az + dz) % 8 * 8 + (ax + r // 2) % 4 * 2 + (ac + r) % 2
 
     def each_ma(body):
-        for dz in FAR:
-            @pl.loop(1 if dz == 0 else 0, 8)
-            def _(r, dz=dz):
+        @pl.loop(0, 8)
+        def _(r):
+            for dz in FAR[:-1]:
                 body(dz * 8 + r, peer(dz, r))
+
+        @pl.loop(1, 8)
+        def _(r):
+            body(r, peer(0, r))
 
     barrier = pltpu.get_barrier_semaphore()
 
@@ -150,8 +155,9 @@
     crecv[:, me] = csend[:, me]
 
     loads[3].wait()
+    loads[8].wait()
     turned = sv[...].astype(F32).T.astype(BF)
-    wide = jnp.broadcast_to(bias_ref[...], (LANES, C)).T
+    wide = jnp.broadcast_to(bv[...], (LANES, C)).T
     bias = jnp.concatenate([wide, wide], axis=1)
     for h in range(rows):
         sk = [dot(turned, xv[b, h]) + bias for b in range(bl)]
@@ -254,7 +260,7 @@
     first, down, up, last = packed_tables(H, W, KX, KY, n, nb)
     fields = fields.transpose(0, 1, 3, 2)
     vmem = pl.BlockSpec(memory_space=pltpu.VMEM)
-    hbm = pl.BlockSpec(memory_space=pl.ANY)
+    hbm = pl.BlockSpec(memory_space=pltpu.HBM)
     tiles = bl * C // LANES
     ma_block = pltpu.VMEM((tiles, n, 2 * rows, LANES), BF)
     ba_block = pltpu.VMEM((tiles, nb, PAD, LANES), BF)
@@ -268,20 +274,23 @@
             jax.ShapeDtypeStruct((tiles, LANES, rows * W), F32),
             jax.ShapeDtypeStruct(last.shape, BF),
         ),
-        in_specs=[hbm, hbm, hbm, hbm, vmem, hbm, hbm, hbm, hbm],
+        in_specs=[hbm] * 9,
         out_specs=(vmem, vmem, vmem),
         scratch_shapes=[
             pltpu.VMEM(fields.shape, BF), pltpu.VMEM(first.shape, BF), pltpu.VMEM(down.shape, BF),
-            pltpu.VMEM(up.shape, BF), pltpu.VMEM((2, modes, C, C), BF), pltpu.VMEM((C, C), BF),
+            pltpu.VMEM(up.shape, BF), pltpu.VMEM((2, modes, C, C), BF), pltpu.VMEM((C, C), BF), pltpu.VMEM((1, C), F32),
             ma_block, ma_block, ba_block, ba_block, mix_block, mix_block, ba_block, ba_block, ma_block,
-            dma((8,)), dma((ng, n)), dma((ng, n)), dma((ng, nb)), dma((ng, nb)), dma((ng, nb)),
+            dma((9,)), dma((ng, n)), dma((ng, n)), dma((ng, nb)), dma((ng, nb)), dma((ng, nb)),
             dma((ng, nb)), dma((ng, n)), dma((ng, n)),
         ],
         compiler_params=pltpu.CompilerParams(
-            collective_id=0, has_side_effects=True, vmem_limit_bytes=48 * 2**20
+            collective_id=0, has_side_effects=True, vmem_limit_bytes=20 * 2**20
         ),
         name="spectral",
-    )(fields, weight_real, weight_imag, skip_weight, out_bias.reshape(1, C), first, down, up, last)
+    )(*[
+        pltpu.with_memory_space_constraint(a, pltpu.HBM)
+        for a in (fields, weight_real, weight_imag, skip_weight, out_bias.reshape(1, C), first, down, up, last)
+    ])
     out = pl.pallas_call(
         final_kernel,
         out_shape=jax.ShapeDtypeStruct(fields.shape, BF),

time: 70.4 us -> 58.6 us (0.83)
  local copies, waits for them, and re-layouts: 8.45 us -> 0 us
  Pallas kernels: 61.6 us -> 58.5 us
    unnamed x16 -> x0, local copies, waits for them, and re-layouts: 8.45 us -> none
    pallas_call x1, Pallas kernels: 59.8 us -> 56.8 us  [kernels(): pl.pallas_call(functools.partial(spectral_kernel, n, nb, GROUPS), out_sha...]
where the time goes in v2:
time: 58.6 us; the launch traced here: 58.5 us
  Pallas kernels  58.5 us (100%)
    pallas_call x1, Pallas kernels, kernels(): pl.pallas_call(functools.partial(spectral_kernel, n, nb, GROUPS), out_sha...  56.8 us
    pallas_call x1, Pallas kernels, kernels(): pl.pallas_call(final_kernel, out_shape=jax.ShapeDtypeStruct(fields.shape,...  1.73 us

profile of v2, /device:TPU:1, one launch (start us, length us, event | category | flops | bytes accessed | tf_op | source)
XLA Modules:
  0.0 58.5 jit_solution(11740213407633311317)
XLA Ops:
  0.0 56.8 %spectral.1 = (bf16[3,64,8,128]{3,2,1,0:T(8,128)(2,1)S(1)}, f32[3,128,1024]{2,1,0:T(8,128)S(1)}, bf16[512,1024]{1,0:T(8,128)(2,1)S(1)}) custom-call(bf16[2,4,192,256]{3,2,1,0:T(8,128)(2,1)} %bitcast.3, bf16[14,1,192,192]{3,2,1,0:T(8,128)(2,1)} %wr_ref.1, bf16[14,1,192,192]{3,2,1,0:T(8,128)(2,1)} %wi_ref.1, bf16[192,192]{1,0:T(8,128)(2,1)} %skip_ref.1, ...), custom_call_target="tpu_custom_call" | custom-call | tf_op jit(solution)/shard_map/spectral/pallas_call | solution.py:270
  56.8 1.7 %finish.1 = bf16[2,4,192,256]{3,2,1,0:T(8,128)(2,1)} custom-call(bf16[3,64,8,128]{3,2,1,0:T(8,128)(2,1)S(1)} %get-tuple-element.8.rr_ref, f32[3,128,1024]{2,1,0:T(8,128)S(1)} %get-tuple-element.9.sk_ref, bf16[512,1024]{1,0:T(8,128)(2,1)S(1)} %get-tuple-element.10.lv_ref), custom_call_target="tpu_custom_call" | custom-call | tf_op jit(solution)/shard_map/finish/pallas_call | solution.py:294

commit v3 on v2

v3 whole, which is shorter than its diff:
```python
import functools
import math

import jax
import jax.numpy as jnp
import numpy as np
from jax import lax
from jax.experimental import pallas as pl
from jax.experimental.pallas import tpu as pltpu
from jax.sharding import PartitionSpec as P

MESH = pl.DeviceIdType.MESH
BF = jnp.bfloat16
F32 = jnp.float32
LANES = 128
HALF = 64
PAD = 16
FAR = (4, 3, 5, 2, 6, 1, 7)


def angles(left, right, extent):
    turn = 2.0 * np.pi / extent * ((left[:, None] * right[None, :]) % extent)
    return np.cos(turn), np.sin(turn)


def packed_tables(H, W, KX, KY, n, nb):
    rows, modes = H // n, KX // nb
    s = 1.0 / math.sqrt(H * W)
    ky = np.arange(KY)
    eye = np.eye(rows)
    cos_w, sin_w = angles(ky, np.arange(W), W)
    g = np.where(ky == 0, 1.0, 2.0)[:, None] * s
    wide = []
    for f in (s, g):
        both = np.stack([cos_w * f, -sin_w * f], 0)
        wide.append(np.einsum("pkw,hg->pkhgw", both, eye).reshape(2 * KY * rows, rows * W))
    i = np.arange(KX)
    kx = np.where(i < KX // 2, i, i + H - KX)
    both = np.stack(angles(kx, np.arange(H), H), 0).reshape(2, nb, modes, H)
    both = np.pad(both, ((0, 0), (0, 0), (0, PAD - modes), (0, 0))).reshape(2, nb * PAD, H)
    down = both.reshape(2 * nb * PAD, H)
    up = both.transpose(0, 2, 1).reshape(2 * H, nb * PAD)
    return [jnp.asarray(a.astype(np.float32)).astype(BF) for a in (wide[0], down, up, wide[1])]


def dot(a, b, over=(1, 0)):
    return lax.dot_general(a, b, (((over[0],), (over[1],)), ((), ())), preferred_element_type=F32)


def lane(a, k):
    return a[:, k * HALF:(k + 1) * HALF]


def side(a, b):
    return jnp.concatenate([a, b], axis=1)


def turn(both, sign):
    m = both.shape[0] // 2
    low = lax.broadcasted_iota(jnp.int32, (m, LANES), 1) < HALF
    out = []
    for k in range(both.shape[1] // LANES):
        p, q = both[:m, k * LANES:(k + 1) * LANES], both[m:, k * LANES:(k + 1) * LANES]
        q = side(lane(q, 1), lane(q, 0))
        out.append(p + jnp.where(low, sign * q, -sign * q))
    return out


def last_step(parts, lv_ref, at, sk):
    rt = []
    for r in parts:
        t = r.astype(F32).T.astype(BF)
        rt.append(side(t[:HALF], t[HALF:]))
    v = dot(jnp.concatenate(rt, axis=0), lv_ref[:, at]) + sk
    inner = math.sqrt(2.0 / math.pi) * (v + 0.044715 * (v * v * v))
    return (0.5 * v * (1.0 + jnp.tanh(inner))).astype(BF)


def spectral_kernel(
    n, nb, x_ref, wr_ref, wi_ref, skip_ref, bias_ref, first_ref, down_ref, up_ref, last_ref,
    done_ref, rr_ref, sk_ref, lv_ref,
    xv, fv, dv, uv, wv, sv, bv, csend, crecv, ysend, yrecv, m1, mo, zsend, zrecv, rsend, rr0, sk0,
    lsem, send_sem, recv_sem,
):
    bl, rows, C, W = x_ref.shape
    modes = wr_ref.shape[0]
    parts = C // HALF
    me = lax.axis_index("ma")
    mine = lax.axis_index("ba")
    az, ax, ac = me // 8, (me // 2) % 4, me % 2

    loads = [
        pltpu.make_async_copy(a, b, lsem.at[k]) for k, (a, b) in enumerate((
            (x_ref, xv), (first_ref, fv), (down_ref, dv), (skip_ref, sv),
            (wr_ref.at[:, 0], wv.at[0]), (wi_ref.at[:, 0], wv.at[1]), (up_ref, uv), (last_ref, lv_ref),
            (bias_ref, bv),
        ))
    ]
    for c in loads:
        c.start()

    def peer(dz, r):
        return (az + dz) % 8 * 8 + (ax + r // 2) % 4 * 2 + (ac + r) % 2

    def each_ma(body):
        @pl.loop(0, 8)
        def _(r):
            for dz in FAR:
                body(peer(dz, r))

        @pl.loop(1, 8)
        def _(r):
            body(peer(0, r))

    def each_ba(body):
        for j in (4, 3, 5, 2, 6, 1, 7):
            body((mine + j) % nb)

    barrier = pltpu.get_barrier_semaphore()
    each_ma(lambda to: pl.semaphore_signal(barrier, inc=1, device_id={"ma": to}, device_id_type=MESH))
    each_ba(lambda to: pl.semaphore_signal(barrier, inc=1, device_id={"ba": to}, device_id_type=MESH))

    zrecv[:, :, modes:, :] = jnp.zeros((bl * parts, nb, PAD - modes, LANES), BF)

    def group(ref, b):
        return ref if ref.shape[0] == parts else ref.at[parts * b:parts * (b + 1)]

    class Exchange:
        def __init__(self, kind, axis, each, here, count, send, recv, used=None):
            self.kind, self.axis, self.each, self.here, self.count = kind, axis, each, here, count
            self.send, self.recv, self.used = send, recv, used

        def block(self, ref, b, d):
            v = group(ref, b)
            return v.at[:, d] if self.used is None else v.at[:, d, 0:self.used]

        def start(self, b):
            def go(to):
                pltpu.make_async_remote_copy(
                    src_ref=self.block(self.send, b, to), dst_ref=self.block(self.recv[b], b, self.here),
                    send_sem=send_sem.at[self.kind, b], recv_sem=recv_sem.at[self.kind, b],
                    device_id={self.axis: to}, device_id_type=MESH,
                ).start()

            self.each(go)
            self.block(self.recv[b], b, self.here)[...] = self.block(self.send, b, self.here)[...]

        def wait(self, ref, b, sem):
            every = self.block(ref, b, slice(0, self.count))
            pltpu.make_async_copy(every, every, sem.at[self.kind, b]).wait()

        def wait_recv(self, b):
            self.wait(self.recv[b], b, recv_sem)

        def wait_send(self, b):
            self.wait(self.send, b, send_sem)

    cols = Exchange(0, "ma", each_ma, me, n - 1, csend, (crecv, crecv))
    specs = Exchange(1, "ba", each_ba, mine, nb - 1, ysend, (yrecv, yrecv), modes)
    mixed = Exchange(2, "ba", each_ba, mine, nb - 1, zsend, (zrecv, zrecv), modes)
    lines = Exchange(3, "ma", each_ma, me, n - 1, rsend, (rr0, rr_ref))

    loads[0].wait()
    loads[1].wait()
    for b in range(bl):
        both = dot(fv[...], jnp.concatenate([xv[b, h] for h in range(rows)], axis=1), (1, 1))
        re, im = both[:n * rows], both[n * rows:]
        for k in range(parts):
            csend[b * parts + k] = side(lane(re, k), lane(im, k)).astype(BF).reshape(n, rows, LANES)
        if b == 0:
            pl.semaphore_wait(barrier, n - 1 + nb - 1)
        cols.start(b)

    loads[3].wait()
    loads[8].wait()
    turned = sv[...].astype(F32).T.astype(BF)
    wide = jnp.broadcast_to(bv[...], (LANES, C)).T
    bias = jnp.concatenate([wide, wide], axis=1)
    for b in range(bl):
        for h in range(rows):
            (sk0, sk_ref)[b][:, h * W:(h + 1) * W] = dot(turned, xv[b, h]) + bias

    def rows_down(b):
        cols.wait_recv(b)
        col = jnp.concatenate([crecv[b * parts + k].reshape(n * rows, LANES) for k in range(parts)], axis=1)
        for k, v in enumerate(turn(dot(dv[...], col), 1.0)):
            ysend[b * parts + k] = v.astype(BF).reshape(nb, PAD, LANES)
        specs.start(b)

    def mix(b):
        specs.wait_recv(b)
        for k in range(parts):
            m1[k] = yrecv[b * parts + k].reshape(nb * PAD, LANES).astype(F32)
        for i in range(modes):
            at = pl.ds(i, nb, stride=PAD)
            v = [m1[k, at, :] for k in range(parts)]
            re, im = [jnp.concatenate([lane(a, p) for a in v], axis=1) for p in range(2)]
            a1 = jnp.concatenate([re, im], axis=0).astype(BF)
            a2 = jnp.concatenate([-im, re], axis=0).astype(BF)
            o = dot(a1, wv[0, i]) + dot(a2, wv[1, i])
            for k in range(parts):
                mo[k, at, :] = side(lane(o[:nb], k), lane(o[nb:], k))
        for k in range(parts):
            zsend[b * parts + k] = mo[k].astype(BF).reshape(nb, PAD, LANES)
        mixed.start(b)

    def rows_up(b):
        mixed.wait_recv(b)
        z = jnp.concatenate([zrecv[b * parts + k].reshape(nb * PAD, LANES) for k in range(parts)], axis=1)
        for k, v in enumerate(turn(dot(uv[...], z), -1.0)):
            rsend[b * parts + k] = v.astype(BF).reshape(n, rows, LANES)
        lines.start(b)

    loads[2].wait()
    rows_down(0)
    rows_down(1)
    loads[4].wait()
    loads[5].wait()
    mix(0)
    mix(1)
    loads[6].wait()
    rows_up(0)
    rows_up(1)
    loads[7].wait()
    for e in (cols, specs, mixed):
        for b in range(bl):
            e.wait_send(b)
    lines.wait_recv(0)
    for h in range(rows):
        at = slice(h * W, (h + 1) * W)
        done_ref[h] = last_step([rr0[k].reshape(n * rows, LANES) for k in range(parts)], lv_ref, at, sk0[:, at])
    lines.wait_recv(1)
    for b in range(bl):
        lines.wait_send(b)


def final_kernel(done_ref, rr_ref, sk_ref, lv_ref, out_ref, ov, sems):
    bl, rows, C, W = out_ref.shape
    parts = C // HALF
    copies = [pltpu.make_async_copy(done_ref, out_ref.at[0], sems.at[rows])]
    copies[0].start()
    r = [rr_ref[k].reshape(-1, LANES) for k in range(parts)]
    for h in range(rows):
        at = slice(h * W, (h + 1) * W)
        ov[h] = last_step(r, lv_ref, at, sk_ref[:, at])
        c = pltpu.make_async_copy(ov.at[h], out_ref.at[1, h], sems.at[h])
        c.start()
        copies.append(c)
    for c in copies:
        c.wait()


def kernels(n, nb, H, KX, KY, fields, weight_real, weight_imag, skip_weight, out_bias):
    bl, rows, W, C = fields.shape
    modes = weight_real.shape[0]
    first, down, up, last = packed_tables(H, W, KX, KY, n, nb)
    fields = fields.transpose(0, 1, 3, 2)
    vmem = pl.BlockSpec(memory_space=pltpu.VMEM)
    hbm = pl.BlockSpec(memory_space=pltpu.HBM)
    parts = C // HALF
    half_block = (parts, n, rows, LANES)
    skip_block = (C, rows * W)
    ma_block = pltpu.VMEM((bl * parts, n, rows, LANES), BF)
    ba_block = pltpu.VMEM((bl * parts, nb, PAD, LANES), BF)
    mix_block = pltpu.VMEM((parts, nb * PAD, LANES), F32)
    dma = pltpu.SemaphoreType.DMA
    half = pl.pallas_call(
        functools.partial(spectral_kernel, n, nb),
        out_shape=(
            jax.ShapeDtypeStruct(fields.shape[1:], BF),
            jax.ShapeDtypeStruct(half_block, BF),
            jax.ShapeDtypeStruct(skip_block, F32),
            jax.ShapeDtypeStruct(last.shape, BF),
        ),
        in_specs=[hbm] * 9,
        out_specs=(vmem,) * 4,
        scratch_shapes=[
            pltpu.VMEM(fields.shape, BF), pltpu.VMEM(first.shape, BF), pltpu.VMEM(down.shape, BF),
            pltpu.VMEM(up.shape, BF), pltpu.VMEM((2, modes, C, C), BF), pltpu.VMEM((C, C), BF),
            pltpu.VMEM((1, C), F32), ma_block, ma_block, ba_block, ba_block, mix_block, mix_block,
            ba_block, ba_block, ma_block, pltpu.VMEM(half_block, BF), pltpu.VMEM(skip_block, F32),
            dma((9,)), dma((4, bl)), dma((4, bl)),
        ],
        compiler_params=pltpu.CompilerParams(
            collective_id=0, has_side_effects=True, vmem_limit_bytes=24 * 2**20
        ),
        name="spectral",
    )(*[
        pltpu.with_memory_space_constraint(a, pltpu.HBM)
        for a in (fields, weight_real, weight_imag, skip_weight, out_bias.reshape(1, C), first, down, up, last)
    ])
    out = pl.pallas_call(
        final_kernel,
        out_shape=jax.ShapeDtypeStruct(fields.shape, BF),
        in_specs=[vmem] * 4,
        out_specs=hbm,
        scratch_shapes=[pltpu.VMEM(fields.shape[1:], BF), dma((rows + 1,))],
        compiler_params=pltpu.CompilerParams(vmem_limit_bytes=16 * 2**20),
        name="finish",
    )(*half)
    return out.transpose(0, 1, 3, 2)


def solution(mesh):
    n, nb = mesh.shape["ma"], mesh.shape["ba"]

    def local(fields, weight_real, weight_imag, skip_weight, out_bias):
        sizes = (fields.shape[1] * n, weight_real.shape[0] * nb, weight_real.shape[1] * n)
        return kernels(n, nb, *sizes, fields, weight_real, weight_imag, skip_weight, out_bias)

    split = P("ba", "ma", None, None)
    return jax.shard_map(
        local, mesh=mesh, in_specs=(split, split, split, P(), P()), out_specs=split, check_vma=False
    )
```

time: 58.6 us -> 49.6 us (0.85)
  Pallas kernels: 58.5 us -> 49.5 us
    pallas_call x1, Pallas kernels: 56.8 us -> 48.2 us  [kernels(): pl.pallas_call(functools.partial(spectral_kernel, n, nb), out_shape=(jax....]
where the time goes in v3:
time: 49.6 us; the launch traced here: 49.5 us
  Pallas kernels  49.5 us (100%)
    pallas_call x1, Pallas kernels, kernels(): pl.pallas_call(functools.partial(spectral_kernel, n, nb), out_shape=(jax....  48.2 us
    pallas_call x1, Pallas kernels, kernels(): pl.pallas_call(final_kernel, out_shape=jax.ShapeDtypeStruct(fields.shape,...  1.27 us

profile of v3, /device:TPU:1, one launch (start us, length us, event | category | flops | bytes accessed | tf_op | source)
XLA Modules:
  0.0 49.5 jit_solution(11625857966451551672)
XLA Ops:
  0.0 48.2 %spectral.1 = (bf16[4,192,256]{2,1,0:T(8,128)(2,1)S(1)}, bf16[3,64,4,128]{3,2,1,0:T(4,128)(2,1)S(1)}, f32[192,1024]{1,0:T(8,128)S(1)}, bf16[512,1024]{1,0:T(8,128)(2,1)S(1)}) custom-call(bf16[2,4,192,256]{3,2,1,0:T(8,128)(2,1)} %bitcast.3, bf16[14,1,192,192]{3,2,1,0:T(8,128)(2,1)} %wr_ref.1, bf16[14,1,192,192]{3,2,1,0:T(8,128)(2,1)} %wi_ref.1, ...), custom_call_target="tpu_custom_call" | custom-call | tf_op jit(solution)/shard_map/spectral/pallas_call | solution.py:267
  48.2 1.3 %finish.1 = bf16[2,4,192,256]{3,2,1,0:T(8,128)(2,1)} custom-call(bf16[4,192,256]{2,1,0:T(8,128)(2,1)S(1)} %get-tuple-element.9.done_ref, bf16[3,64,4,128]{3,2,1,0:T(4,128)(2,1)S(1)} %get-tuple-element.10.rr_ref, f32[192,1024]{1,0:T(8,128)S(1)} %get-tuple-element.11.sk_ref, bf16[512,1024]{1,0:T(8,128)(2,1)S(1)} %get-tuple-element.12.lv_ref), custom_call_target="tpu_custom_call" | custom-call | tf_op jit(solution)/shard_map/finish/pallas_call | solution.py:292

commit v4 on v3

--- a/solution.py
+++ b/solution.py
@@ -15,7 +15,18 @@
 LANES = 128
 HALF = 64
 PAD = 16
-FAR = (4, 3, 5, 2, 6, 1, 7)
+TURNS = (4, 5, 3, 6, 2, 7, 1)
+
+
+def offsets():
+    out = [
+        (dz, dx, dc) for dc in (1, 0) for dxs in ((2,), (1, 3), (0,)) for dz in TURNS for dx in dxs
+    ]
+    return out + [(0, dx, dc) for dx, dc in ((2, 1), (2, 0), (1, 1), (3, 1), (1, 0), (3, 0), (0, 1))]
+
+
+def hops(o):
+    return min(o[0], 8 - o[0]) + min(o[1], 4 - o[1])
 
 
 def angles(left, right, extent):
@@ -66,14 +77,19 @@
     return out
 
 
-def last_step(parts, lv_ref, at, sk):
-    rt = []
+def turned_lines(parts):
+    out = []
     for r in parts:
         t = r.astype(F32).T.astype(BF)
-        rt.append(side(t[:HALF], t[HALF:]))
-    v = dot(jnp.concatenate(rt, axis=0), lv_ref[:, at]) + sk
-    inner = math.sqrt(2.0 / math.pi) * (v + 0.044715 * (v * v * v))
-    return (0.5 * v * (1.0 + jnp.tanh(inner))).astype(BF)
+        out.append(side(t[:HALF], t[HALF:]))
+    return jnp.concatenate(out, axis=0)
+
+
+def last_step(rt, lv_ref, at, sk):
+    v = dot(rt, lv_ref[:, at]) + sk
+    c = math.sqrt(2.0 / math.pi)
+    half = 0.5 * v
+    return (half + half * jnp.tanh(v * (c + (0.044715 * c) * (v * v)))).astype(BF)
 
 
 def spectral_kernel(
@@ -99,25 +115,20 @@
     for c in loads:
         c.start()
 
-    def peer(dz, r):
-        return (az + dz) % 8 * 8 + (ax + r // 2) % 4 * 2 + (ac + r) % 2
+    def peer(dz, dx, dc):
+        return (az + dz) % 8 * 8 + (ax + dx) % 4 * 2 + (ac + dc) % 2
 
     def each_ma(body):
-        @pl.loop(0, 8)
-        def _(r):
-            for dz in FAR:
-                body(peer(dz, r))
-
-        @pl.loop(1, 8)
-        def _(r):
-            body(peer(0, r))
+        for o in offsets():
+            body(peer(*o))
 
     def each_ba(body):
         for j in (4, 3, 5, 2, 6, 1, 7):
             body((mine + j) % nb)
 
     barrier = pltpu.get_barrier_semaphore()
-    each_ma(lambda to: pl.semaphore_signal(barrier, inc=1, device_id={"ma": to}, device_id_type=MESH))
+    for o in sorted(offsets(), key=lambda o: -hops(o)):
+        pl.semaphore_signal(barrier, inc=1, device_id={"ma": peer(*o)}, device_id_type=MESH)
     each_ba(lambda to: pl.semaphore_signal(barrier, inc=1, device_id={"ba": to}, device_id_type=MESH))
 
     zrecv[:, :, modes:, :] = jnp.zeros((bl * parts, nb, PAD - modes, LANES), BF)
@@ -226,9 +237,10 @@
         for b in range(bl):
             e.wait_send(b)
     lines.wait_recv(0)
+    rt = turned_lines([rr0[k].reshape(n * rows, LANES) for k in range(parts)])
     for h in range(rows):
         at = slice(h * W, (h + 1) * W)
-        done_ref[h] = last_step([rr0[k].reshape(n * rows, LANES) for k in range(parts)], lv_ref, at, sk0[:, at])
+        done_ref[h] = last_step(rt, lv_ref, at, sk0[:, at])
     lines.wait_recv(1)
     for b in range(bl):
         lines.wait_send(b)
@@ -239,10 +251,10 @@
     parts = C // HALF
     copies = [pltpu.make_async_copy(done_ref, out_ref.at[0], sems.at[rows])]
     copies[0].start()
-    r = [rr_ref[k].reshape(-1, LANES) for k in range(parts)]
+    rt = turned_lines([rr_ref[k].reshape(-1, LANES) for k in range(parts)])
     for h in range(rows):
         at = slice(h * W, (h + 1) * W)
-        ov[h] = last_step(r, lv_ref, at, sk_ref[:, at])
+        ov[h] = last_step(rt, lv_ref, at, sk_ref[:, at])
         c = pltpu.make_async_copy(ov.at[h], out_ref.at[1, h], sems.at[h])
         c.start()
         copies.append(c)

time: 49.6 us -> 47.2 us (0.952)
  Pallas kernels: 49.5 us -> 47.1 us
    pallas_call x1, Pallas kernels: 48.2 us -> 45.9 us  [kernels(): pl.pallas_call(functools.partial(spectral_kernel, n, nb), out_shape=(jax....]
where the time goes in v4:
time: 47.2 us; the launch traced here: 47.1 us
  Pallas kernels  47.1 us (100%)
    pallas_call x1, Pallas kernels, kernels(): pl.pallas_call(functools.partial(spectral_kernel, n, nb), out_shape=(jax....  45.9 us
    pallas_call x1, Pallas kernels, kernels(): pl.pallas_call(final_kernel, out_shape=jax.ShapeDtypeStruct(fields.shape,...  1.25 us

profile of v4, /device:TPU:1, one launch (start us, length us, event | category | flops | bytes accessed | tf_op | source)
XLA Modules:
  0.0 47.1 jit_solution(5572929671697478646)
XLA Ops:
  0.0 45.9 %spectral.1 = (bf16[4,192,256]{2,1,0:T(8,128)(2,1)S(1)}, bf16[3,64,4,128]{3,2,1,0:T(4,128)(2,1)S(1)}, f32[192,1024]{1,0:T(8,128)S(1)}, bf16[512,1024]{1,0:T(8,128)(2,1)S(1)}) custom-call(bf16[2,4,192,256]{3,2,1,0:T(8,128)(2,1)} %bitcast.3, bf16[14,1,192,192]{3,2,1,0:T(8,128)(2,1)} %wr_ref.1, bf16[14,1,192,192]{3,2,1,0:T(8,128)(2,1)} %wi_ref.1, ...), custom_call_target="tpu_custom_call" | custom-call | tf_op jit(solution)/shard_map/spectral/pallas_call | solution.py:279
  45.9 1.2 %finish.1 = bf16[2,4,192,256]{3,2,1,0:T(8,128)(2,1)} custom-call(bf16[4,192,256]{2,1,0:T(8,128)(2,1)S(1)} %get-tuple-element.9.done_ref, bf16[3,64,4,128]{3,2,1,0:T(4,128)(2,1)S(1)} %get-tuple-element.10.rr_ref, f32[192,1024]{1,0:T(8,128)S(1)} %get-tuple-element.11.sk_ref, bf16[512,1024]{1,0:T(8,128)(2,1)S(1)} %get-tuple-element.12.lv_ref), custom_call_target="tpu_custom_call" | custom-call | tf_op jit(solution)/shard_map/finish/pallas_call | solution.py:304

commit v5 on v4

--- a/solution.py
+++ b/solution.py
@@ -15,6 +15,7 @@
 LANES = 128
 HALF = 64
 PAD = 16
+PLAN = ((0, 0), (0, 1), (1, 0), (0, 2), (1, 1), (1, 2))
 TURNS = (4, 5, 3, 6, 2, 7, 1)
 
 
@@ -23,6 +24,14 @@
         (dz, dx, dc) for dc in (1, 0) for dxs in ((2,), (1, 3), (0,)) for dz in TURNS for dx in dxs
     ]
     return out + [(0, dx, dc) for dx, dc in ((2, 1), (2, 0), (1, 1), (3, 1), (1, 0), (3, 0), (0, 1))]
+
+
+def ring(group):
+    xs = ((2,), (1, 3), (0,))[group]
+    out = [(dz, dx, dc) for dc in (1, 0) for dz in TURNS for dx in xs]
+    if group == 2:
+        out += [o for o in offsets() if o[0] == 0]
+    return out
 
 
 def hops(o):
@@ -118,8 +127,8 @@
     def peer(dz, dx, dc):
         return (az + dz) % 8 * 8 + (ax + dx) % 4 * 2 + (ac + dc) % 2
 
-    def each_ma(body):
-        for o in offsets():
+    def each_ma(body, order=None):
+        for o in order or offsets():
             body(peer(*o))
 
     def each_ba(body):
@@ -145,7 +154,7 @@
             v = group(ref, b)
             return v.at[:, d] if self.used is None else v.at[:, d, 0:self.used]
 
-        def start(self, b):
+        def start(self, b, *order):
             def go(to):
                 pltpu.make_async_remote_copy(
                     src_ref=self.block(self.send, b, to), dst_ref=self.block(self.recv[b], b, self.here),
@@ -153,7 +162,9 @@
                     device_id={self.axis: to}, device_id_type=MESH,
                 ).start()
 
-            self.each(go)
+            self.each(go, *order)
+
+        def keep(self, b):
             self.block(self.recv[b], b, self.here)[...] = self.block(self.send, b, self.here)[...]
 
         def wait(self, ref, b, sem):
@@ -178,9 +189,11 @@
         re, im = both[:n * rows], both[n * rows:]
         for k in range(parts):
             csend[b * parts + k] = side(lane(re, k), lane(im, k)).astype(BF).reshape(n, rows, LANES)
-        if b == 0:
-            pl.semaphore_wait(barrier, n - 1 + nb - 1)
-        cols.start(b)
+    pl.semaphore_wait(barrier, n - 1 + nb - 1)
+    for b, k in PLAN:
+        cols.start(b, ring(k))
+    for b in range(bl):
+        cols.keep(b)
 
     loads[3].wait()
     loads[8].wait()
@@ -197,6 +210,7 @@
         for k, v in enumerate(turn(dot(dv[...], col), 1.0)):
             ysend[b * parts + k] = v.astype(BF).reshape(nb, PAD, LANES)
         specs.start(b)
+        specs.keep(b)
 
     def mix(b):
         specs.wait_recv(b)
@@ -214,6 +228,7 @@
         for k in range(parts):
             zsend[b * parts + k] = mo[k].astype(BF).reshape(nb, PAD, LANES)
         mixed.start(b)
+        mixed.keep(b)
 
     def rows_up(b):
         mixed.wait_recv(b)
@@ -221,6 +236,7 @@
         for k, v in enumerate(turn(dot(uv[...], z), -1.0)):
             rsend[b * parts + k] = v.astype(BF).reshape(n, rows, LANES)
         lines.start(b)
+        lines.keep(b)
 
     loads[2].wait()
     rows_down(0)

time: 47.2 us -> 47 us (level)
  no operation moved by 1% of the time
where the time goes in v5:
time: 47 us; the launch traced here: 46.9 us
  Pallas kernels  46.9 us (100%)
    pallas_call x1, Pallas kernels, kernels(): pl.pallas_call(functools.partial(spectral_kernel, n, nb), out_shape=(jax....  45.6 us
    pallas_call x1, Pallas kernels, kernels(): pl.pallas_call(final_kernel, out_shape=jax.ShapeDtypeStruct(fields.shape,...  1.25 us

profile of v5, /device:TPU:1, one launch (start us, length us, event | category | flops | bytes accessed | tf_op | source)
XLA Modules:
  0.0 46.9 jit_solution(18423493029492223582)
XLA Ops:
  0.0 45.6 %spectral.1 = (bf16[4,192,256]{2,1,0:T(8,128)(2,1)S(1)}, bf16[3,64,4,128]{3,2,1,0:T(4,128)(2,1)S(1)}, f32[192,1024]{1,0:T(8,128)S(1)}, bf16[512,1024]{1,0:T(8,128)(2,1)S(1)}) custom-call(bf16[2,4,192,256]{3,2,1,0:T(8,128)(2,1)} %bitcast.3, bf16[14,1,192,192]{3,2,1,0:T(8,128)(2,1)} %wr_ref.1, bf16[14,1,192,192]{3,2,1,0:T(8,128)(2,1)} %wi_ref.1, ...), custom_call_target="tpu_custom_call" | custom-call | tf_op jit(solution)/shard_map/spectral/pallas_call | solution.py:295
  45.6 1.2 %finish.1 = bf16[2,4,192,256]{3,2,1,0:T(8,128)(2,1)} custom-call(bf16[4,192,256]{2,1,0:T(8,128)(2,1)S(1)} %get-tuple-element.9.done_ref, bf16[3,64,4,128]{3,2,1,0:T(4,128)(2,1)S(1)} %get-tuple-element.10.rr_ref, f32[192,1024]{1,0:T(8,128)S(1)} %get-tuple-element.11.sk_ref, bf16[512,1024]{1,0:T(8,128)(2,1)S(1)} %get-tuple-element.12.lv_ref), custom_call_target="tpu_custom_call" | custom-call | tf_op jit(solution)/shard_map/finish/pallas_call | solution.py:320

commit v6 on v5

--- a/solution.py
+++ b/solution.py
@@ -16,7 +16,7 @@
 HALF = 64
 PAD = 16
 PLAN = ((0, 0), (0, 1), (1, 0), (0, 2), (1, 1), (1, 2))
-TURNS = (4, 5, 3, 6, 2, 7, 1)
+TURNS = (4, 3, 5, 2, 6, 1, 7)
 
 
 def offsets():

time: 47 us -> 47.1 us (level)
  no operation moved by 1% of the time
where the time goes in v6:
time: 47.1 us; the launch traced here: 47 us
  Pallas kernels  47 us (100%)
    pallas_call x1, Pallas kernels, kernels(): pl.pallas_call(functools.partial(spectral_kernel, n, nb), out_shape=(jax....  45.7 us
    pallas_call x1, Pallas kernels, kernels(): pl.pallas_call(final_kernel, out_shape=jax.ShapeDtypeStruct(fields.shape,...  1.25 us

profile of v6, /device:TPU:1, one launch (start us, length us, event | category | flops | bytes accessed | tf_op | source)
XLA Modules:
  0.0 47.0 jit_solution(13172303385381424028)
XLA Ops:
  0.0 45.7 %spectral.1 = (bf16[4,192,256]{2,1,0:T(8,128)(2,1)S(1)}, bf16[3,64,4,128]{3,2,1,0:T(4,128)(2,1)S(1)}, f32[192,1024]{1,0:T(8,128)S(1)}, bf16[512,1024]{1,0:T(8,128)(2,1)S(1)}) custom-call(bf16[2,4,192,256]{3,2,1,0:T(8,128)(2,1)} %bitcast.3, bf16[14,1,192,192]{3,2,1,0:T(8,128)(2,1)} %wr_ref.1, bf16[14,1,192,192]{3,2,1,0:T(8,128)(2,1)} %wi_ref.1, ...), custom_call_target="tpu_custom_call" | custom-call | tf_op jit(solution)/shard_map/spectral/pallas_call | solution.py:295
  45.7 1.2 %finish.1 = bf16[2,4,192,256]{3,2,1,0:T(8,128)(2,1)} custom-call(bf16[4,192,256]{2,1,0:T(8,128)(2,1)S(1)} %get-tuple-element.9.done_ref, bf16[3,64,4,128]{3,2,1,0:T(4,128)(2,1)S(1)} %get-tuple-element.10.rr_ref, f32[192,1024]{1,0:T(8,128)S(1)} %get-tuple-element.11.sk_ref, bf16[512,1024]{1,0:T(8,128)(2,1)S(1)} %get-tuple-element.12.lv_ref), custom_call_target="tpu_custom_call" | custom-call | tf_op jit(solution)/shard_map/finish/pallas_call | solution.py:320
